TPU v7x, 256 devices: a whole 4x4x8 slice. The times are simulated.
256 devices in a mesh: mp: 64 (over y, z, core), dp: 4 (over x).
Axes of the slice: x: 4, y: 4, z: 8, core: 2. Of those that a mesh axis runs over, the one named last changes fastest.
Arguments:
- features: bfloat16 [256, 4, 4, 512], P(('dp', 'mp')), may hold values from 0 to 2
- labels: int32 [256], P('dp'), may hold values from 0 to 9
- subset_ids: int32 [64], P('mp'), may hold values from 0 to 255
- conv1_weight: bfloat16 [64, 9, 512, 512], P('mp'), may hold values from -0.09375 to 0.09375
- conv2_weight: bfloat16 [64, 9, 512, 512], P('mp'), may hold values from -0.09375 to 0.09375
- head_weight: float32 [64, 512, 10], P('mp'), may hold values from -0.25 to 0.25
Outputs:
- datamodel: float32 [256, 256], P(('dp', 'mp'))
- margin_mean: float32 [256], P(('dp', 'mp'))
- margin_norm: float32 [256], P(('dp', 'mp'))
All inputs are finite; a program needn't handle non-finite values.
Results may differ from a plain program's by a relative error of at most 0.00077.
Values may be sent and summed in bfloat16 or wider, within the bound.
No kernel may reach another device: no remote copies, remote signals or barrier semaphores. Data moves between devices by JAX's collectives and lax.ppermute only.
A program may use at most 128 MiB of HBM per device.

v0:
```python
import jax
import jax.numpy as jnp
from jax import lax
from jax.sharding import PartitionSpec as P

SUBSETS = 256


def in_order(pieces, dim):
    pieces = jnp.moveaxis(pieces, 0, dim)
    dims = pieces.shape
    return pieces.reshape(*dims[:dim], dims[dim] * dims[dim + 1], *dims[dim + 2 :])


def sent_to_all(x, axis):
    devices = lax.axis_size(axis)
    return lax.all_to_all(jnp.broadcast_to(x[None], (devices, *x.shape)), axis, 0, 0, tiled=True)


def gathered_copies(x, axis, dim):
    return in_order(sent_to_all(x, axis), dim)


def convolve(grid, kernel):
    batch = grid.shape[0]
    width = grid.shape[1]
    chans = grid.shape[3]
    padded = jnp.pad(grid, ((0, 0), (1, 1), (1, 1), (0, 0)))
    result = jnp.zeros((batch * width * width, kernel.shape[2]), jnp.float32)
    for offset in range(9):
        row_off, col_off = divmod(offset, 3)
        shifted = padded[:, row_off : row_off + width, col_off : col_off + width, :].reshape(
            batch * width * width, chans
        )
        result = result + jnp.dot(shifted, kernel[offset], preferred_element_type=jnp.float32)
    return result


def margins_of(grid, first_kernel, second_kernel, head, target_labels):
    batch = grid.shape[0]
    width = grid.shape[1]
    chans = grid.shape[3]
    hidden = (
        jax.nn.relu(convolve(grid, first_kernel))
        .astype(jnp.bfloat16)
        .reshape(batch, width, width, chans)
    )
    branch = jax.nn.relu(convolve(hidden, second_kernel))
    blocked = grid.astype(jnp.float32).reshape(batch * width * width, chans) + branch
    pooled = jnp.max(blocked.reshape(batch, width * width, chans), axis=1)
    logits = jnp.dot(
        pooled, head, precision=lax.Precision.HIGHEST, preferred_element_type=jnp.float32
    )
    classes = jnp.arange(head.shape[1], dtype=jnp.int32)[None, :]
    chosen = classes == target_labels[:, None]
    correct = jnp.sum(jnp.where(chosen, logits, 0.0), axis=1)
    rival = jnp.max(jnp.where(chosen, -1e30, logits), axis=1)
    return correct - rival


def subset_table(identity):
    return (identity[:, None] == jnp.arange(SUBSETS, dtype=jnp.int32)[None, :]).astype(jnp.float32)


def shards(features, labels, subset_ids, conv1_weight, conv2_weight, head_weight):
    models_dev = conv1_weight.shape[0]
    model_count = models_dev * lax.axis_size("mp")
    rows_out = [
        margins_of(
            gathered_copies(features, "mp", 0),
            conv1_weight[0],
            conv2_weight[0],
            head_weight[0],
            labels,
        )
    ]
    margin = jnp.stack(rows_out, 0)
    columns = lax.all_to_all(margin, "mp", split_axis=1, concat_axis=0, tiled=True)
    every_id = gathered_copies(subset_ids, "mp", 0)
    margin_mean = jnp.sum(columns, axis=0) / model_count
    centred = columns - margin_mean[None, :]
    margin_norm = jnp.sqrt(1.0 + jnp.sum(centred * centred, axis=0) / model_count)
    scaled = centred / margin_norm[None, :]
    datamodel = jnp.dot(
        scaled.T,
        subset_table(every_id),
        precision=lax.Precision.HIGHEST,
        preferred_element_type=jnp.float32,
    )
    return (datamodel, margin_mean, margin_norm)


def solution(mesh):
    in_specs = (
        P(("dp", "mp"), None, None, None),
        P("dp"),
        P("mp"),
        P("mp", None, None, None),
        P("mp", None, None, None),
        P("mp", None, None),
    )
    out_specs = (P(("dp", "mp"), None), P(("dp", "mp")), P(("dp", "mp")))
    return jax.shard_map(shards, mesh=mesh, in_specs=in_specs, out_specs=out_specs, check_vma=False)
```

profile of v0, /device:TPU:1, one launch (start us, length us, event | category | flops | bytes accessed | tf_op | source)
XLA Modules:
  0.0 186.4 jit_solution(11144858232999645998)
XLA Ops:
  0.6 2.2 %broadcast_in_dim.30 = bf16[64,1,4,4,512]{4,3,2,1,0:T(4,128)(2,1)} broadcast(bf16[4,4,512]{2,1,0:T(4,128)(2,1)} %bitcast.93), dimensions={2,3,4} | broadcast | bytes 1064960 | tf_op jit(solution)/shard_map/broadcast_in_dim | solution.py:17
  2.8 13.1 %all-to-all-start = ((bf16[64,1,4,4,512]{4,3,2,1,0:T(4,128)(2,1)}), bf16[64,1,4,4,512]{4,3,2,1,0:T(4,128)(2,1)S(1)}, u32[]{:S(2)}, u32[]{:S(2)}) async-start(bf16[64,1,4,4,512]{4,3,2,1,0:T(4,128)(2,1)} %broadcast_in_dim.30), calls=%async_computation | async-start | bytes 2097152 | tf_op jit(solution)/shard_map/all_to_all | solution.py:17
  16.6 27.9 %all-to-all-done = bf16[64,1,4,4,512]{4,3,2,1,0:T(4,128)(2,1)S(1)} async-done(((bf16[64,1,4,4,512]{4,3,2,1,0:T(4,128)(2,1)}), bf16[64,1,4,4,512]{4,3,2,1,0:T(4,128)(2,1)S(1)}, u32[]{:S(2)}, u32[]{:S(2)}) %all-to-all-start) | async-done | bytes 1048608 | tf_op jit(solution)/shard_map/all_to_all | solution.py:17
  44.5 0.6 broadcast_in_dim.34
  45.1 6.2 %all-to-all-start.2 = ((s32[64,1,1]{2,1,0:T(1,128)}), s32[64,1,1]{2,1,0:T(1,128)S(1)}, u32[]{:S(2)}, u32[]{:S(2)}) async-start(s32[64,1,1]{2,1,0:T(1,128)} %broadcast_in_dim.34), calls=%async_computation.2 | async-start | bytes 65536 | tf_op jit(solution)/shard_map/all_to_all | solution.py:17
  51.4 5.8 %pad_slice_fusion.8 = (bf16[64,4,4,512]{3,2,1,0:T(4,128)(2,1)S(1)}, bf16[64,4,4,512]{3,2,1,0:T(4,128)(2,1)}, bf16[64,4,4,512]{3,2,1,0:T(4,128)(2,1)}, bf16[64,4,...) fusion(bf16[64,4,4,512]{3,2,1,0:T(4,128)(2,1)S(1)} %bitcast.92), kind=kLoop, calls=%fused_computation.8 | loop fusion | bytes 9437184 | tf_op jit(solution)/shard_map/slice | solution.py:32
  57.2 2.1 %reshape.190 = bf16[1024,512]{1,0:T(8,128)(2,1)} reshape(bf16[64,4,4,512]{3,2,1,0:T(4,128)(2,1)} %get-tuple-element.19) | data formatting | bytes 2097152 | tf_op jit(solution)/shard_map/reshape | solution.py:32
  59.3 2.2 %reshape.189 = bf16[1024,512]{1,0:T(8,128)(2,1)} reshape(bf16[64,4,4,512]{3,2,1,0:T(4,128)(2,1)} %get-tuple-element.18) | data formatting | bytes 2097152 | tf_op jit(solution)/shard_map/reshape | solution.py:32
  61.5 3.5 %fusion.18 = f32[1024,512]{1,0:T(8,128)} fusion(bf16[1024,512]{1,0:T(8,128)(2,1)} %reshape.190, bf16[1,9,512,512]{3,2,1,0:T(8,128)(2,1)} %param.9), kind=kOutput, calls=%fused_computation.37 | convolution fusion | flops 536870912 | bytes 3670016 | tf_op jit(solution)/shard_map/dot_general | solution.py:35
  65.0 0.0 copy-done.7
  65.0 3.0 %fusion.20 = f32[1024,512]{1,0:T(8,128)} fusion(bf16[1024,512]{1,0:T(8,128)(2,1)S(1)} %copy-done.7, bf16[1,9,512,512]{3,2,1,0:T(8,128)(2,1)} %param.9), kind=kOutput, calls=%fused_computation.39 | convolution fusion | flops 536870912 | bytes 3670016 | tf_op jit(solution)/shard_map/dot_general | solution.py:35
  68.0 2.2 %reshape.188 = bf16[1024,512]{1,0:T(8,128)(2,1)} reshape(bf16[64,4,4,512]{3,2,1,0:T(4,128)(2,1)} %get-tuple-element.17) | data formatting | bytes 2097152 | tf_op jit(solution)/shard_map/reshape | solution.py:32
  70.2 3.4 %fusion.22 = f32[1024,512]{1,0:T(8,128)} fusion(bf16[1024,512]{1,0:T(8,128)(2,1)} %reshape.188, bf16[1,9,512,512]{3,2,1,0:T(8,128)(2,1)} %param.9), kind=kOutput, calls=%fused_computation.41 | convolution fusion | flops 536870912 | bytes 3670016 | tf_op jit(solution)/shard_map/dot_general | solution.py:35
  73.6 2.1 %reshape.187 = bf16[1024,512]{1,0:T(8,128)(2,1)} reshape(bf16[64,4,4,512]{3,2,1,0:T(4,128)(2,1)} %get-tuple-element.16) | data formatting | bytes 2097152 | tf_op jit(solution)/shard_map/reshape | solution.py:32
  75.7 3.4 %fusion.26 = f32[1024,512]{1,0:T(8,128)} fusion(bf16[1024,512]{1,0:T(8,128)(2,1)} %reshape.187, bf16[1,9,512,512]{3,2,1,0:T(8,128)(2,1)} %param.9), kind=kOutput, calls=%fused_computation.45 | convolution fusion | flops 536870912 | bytes 3670016 | tf_op jit(solution)/shard_map/dot_general | solution.py:35
  79.1 2.1 %reshape.186 = bf16[1024,512]{1,0:T(8,128)(2,1)} reshape(bf16[64,4,4,512]{3,2,1,0:T(4,128)(2,1)} %get-tuple-element.15) | data formatting | bytes 2097152 | tf_op jit(solution)/shard_map/reshape | solution.py:32
  81.3 3.5 %fusion.28 = f32[1024,512]{1,0:T(8,128)} fusion(bf16[1024,512]{1,0:T(8,128)(2,1)} %reshape.186, bf16[1,9,512,512]{3,2,1,0:T(8,128)(2,1)} %param.9), kind=kOutput, calls=%fused_computation.47 | convolution fusion | flops 536870912 | bytes 3670016 | tf_op jit(solution)/shard_map/dot_general | solution.py:35
  84.7 2.2 %reshape.185 = bf16[1024,512]{1,0:T(8,128)(2,1)} reshape(bf16[64,4,4,512]{3,2,1,0:T(4,128)(2,1)} %get-tuple-element.14) | data formatting | bytes 2097152 | tf_op jit(solution)/shard_map/reshape | solution.py:32
  86.9 3.4 %fusion.30 = f32[1024,512]{1,0:T(8,128)} fusion(bf16[1024,512]{1,0:T(8,128)(2,1)} %reshape.185, bf16[1,9,512,512]{3,2,1,0:T(8,128)(2,1)} %param.9), kind=kOutput, calls=%fused_computation.49 | convolution fusion | flops 536870912 | bytes 3670016 | tf_op jit(solution)/shard_map/dot_general | solution.py:35
  90.3 1.1 reshape.184
  91.4 3.4 %fusion.32 = f32[1024,512]{1,0:T(8,128)} fusion(bf16[1024,512]{1,0:T(8,128)(2,1)} %reshape.184, bf16[1,9,512,512]{3,2,1,0:T(8,128)(2,1)} %param.9), kind=kOutput, calls=%fused_computation.51 | convolution fusion | flops 536870912 | bytes 3670016 | tf_op jit(solution)/shard_map/dot_general | solution.py:35
  94.8 0.3 reshape.191
  95.1 0.3 reshape.182
  95.4 0.0 copy-start.1
  95.4 1.9 %fusion.24 = f32[1024,512]{1,0:T(8,128)S(1)} fusion(bf16[1024,512]{1,0:T(8,128)(2,1)S(1)} %reshape.182, bf16[1,9,512,512]{3,2,1,0:T(8,128)(2,1)} %param.9), kind=kOutput, calls=%fused_computation.43 | convolution fusion | flops 536870912 | bytes 3670016 | tf_op jit(solution)/shard_map/dot_general | solution.py:35
  97.3 0.0 copy-done.1
  97.3 6.3 %maximum_convert_fusion = bf16[1024,512]{1,0:T(8,128)(2,1)S(1)} fusion(f32[1024,512]{1,0:T(8,128)S(1)} %copy-done.1, f32[1024,512]{1,0:T(8,128)} %fusion.20, f32[1024,512]{1,0:T(8,128)} %fusion.22, f32[1024,512]{1,0:T(8,128)S(1)} %fusion.24, f32[1024,512]{1,0:T(8,128)} %fusion.26, f32[1024,512]{1,0:T(8,128)} %fusion.28, f32[1024,512]{1,0:T(8,128)} %fusion.32, ...), kind=kOutput, calls=%fused_computation.18 | convolution fusion | flops 542113792 | bytes 19398656 | tf_op jit(solution)/shard_map/dot_general | solution.py:35
  103.7 1.1 reshape.192
  104.8 9.1 %pad_slice_fusion = (bf16[64,4,4,512]{3,2,1,0:T(4,128)(2,1)}, bf16[64,4,4,512]{3,2,1,0:T(4,128)(2,1)}, bf16[64,4,4,512]{3,2,1,0:T(4,128)(2,1)}, bf16[64,4,4,512]...) fusion(bf16[64,4,4,512]{3,2,1,0:T(4,128)(2,1)} %reshape.192), kind=kLoop, calls=%fused_computation | loop fusion | bytes 9437184 | tf_op jit(solution)/shard_map/slice | solution.py:32
  113.8 2.2 %reshape.199 = bf16[1024,512]{1,0:T(8,128)(2,1)} reshape(bf16[64,4,4,512]{3,2,1,0:T(4,128)(2,1)} %get-tuple-element.11) | data formatting | bytes 2097152 | tf_op jit(solution)/shard_map/reshape | solution.py:32
  116.0 3.2 %fusion.7 = f32[1024,512]{1,0:T(8,128)} fusion(bf16[1024,512]{1,0:T(8,128)(2,1)S(1)} %maximum_convert_fusion, bf16[1,9,512,512]{3,2,1,0:T(8,128)(2,1)} %param.10), kind=kOutput, calls=%fused_computation.26 | convolution fusion | flops 536870912 | bytes 3670016 | tf_op jit(solution)/shard_map/dot_general | solution.py:35
  119.2 0.0 copy-done.8
  119.2 3.1 %fusion.1 = f32[1024,512]{1,0:T(8,128)} fusion(bf16[1024,512]{1,0:T(8,128)(2,1)S(1)} %copy-done.8, bf16[1,9,512,512]{3,2,1,0:T(8,128)(2,1)} %param.10), kind=kOutput, calls=%fused_computation.20 | convolution fusion | flops 536870912 | bytes 3670016 | tf_op jit(solution)/shard_map/dot_general | solution.py:35
  122.3 0.0 copy-done.6
  122.3 1.1 reshape.195
  123.4 3.5 %fusion.11 = f32[1024,512]{1,0:T(8,128)} fusion(bf16[1024,512]{1,0:T(8,128)(2,1)} %reshape.195, bf16[1,9,512,512]{3,2,1,0:T(8,128)(2,1)} %param.10), kind=kOutput, calls=%fused_computation.30 | convolution fusion | flops 536870912 | bytes 3670016 | tf_op jit(solution)/shard_map/dot_general | solution.py:35
  126.9 0.0 copy-done.5
  126.9 1.2 reshape.194
  128.1 3.5 %fusion.13 = f32[1024,512]{1,0:T(8,128)} fusion(bf16[1024,512]{1,0:T(8,128)(2,1)} %reshape.194, bf16[1,9,512,512]{3,2,1,0:T(8,128)(2,1)} %param.10), kind=kOutput, calls=%fused_computation.32 | convolution fusion | flops 536870912 | bytes 3670016 | tf_op jit(solution)/shard_map/dot_general | solution.py:35
  131.6 0.0 copy-done.4
  131.6 1.1 reshape.193
  132.7 3.5 %fusion.15 = f32[1024,512]{1,0:T(8,128)} fusion(bf16[1024,512]{1,0:T(8,128)(2,1)} %reshape.193, bf16[1,9,512,512]{3,2,1,0:T(8,128)(2,1)} %param.10), kind=kOutput, calls=%fused_computation.34 | convolution fusion | flops 536870912 | bytes 3670016 | tf_op jit(solution)/shard_map/dot_general | solution.py:35
  136.3 0.0 copy-done.3
  136.3 1.1 reshape.198
  137.4 3.4 %fusion.3 = f32[1024,512]{1,0:T(8,128)} fusion(bf16[1024,512]{1,0:T(8,128)(2,1)} %reshape.198, bf16[1,9,512,512]{3,2,1,0:T(8,128)(2,1)} %param.10), kind=kOutput, calls=%fused_computation.22 | convolution fusion | flops 536870912 | bytes 3670016 | tf_op jit(solution)/shard_map/dot_general | solution.py:35
  140.8 0.0 copy-done.2
  140.8 1.1 reshape.197
  141.9 3.4 %fusion.5 = f32[1024,512]{1,0:T(8,128)} fusion(bf16[1024,512]{1,0:T(8,128)(2,1)} %reshape.197, bf16[1,9,512,512]{3,2,1,0:T(8,128)(2,1)} %param.10), kind=kOutput, calls=%fused_computation.24 | convolution fusion | flops 536870912 | bytes 3670016 | tf_op jit(solution)/shard_map/dot_general | solution.py:35
  145.3 1.2 reshape.196
  146.5 3.5 %fusion.9 = f32[1024,512]{1,0:T(8,128)} fusion(bf16[1024,512]{1,0:T(8,128)(2,1)} %reshape.196, bf16[1,9,512,512]{3,2,1,0:T(8,128)(2,1)} %param.10), kind=kOutput, calls=%fused_computation.28 | convolution fusion | flops 536870912 | bytes 3670016 | tf_op jit(solution)/shard_map/dot_general | solution.py:35
  150.0 2.2 %reshape.200 = bf16[1024,512]{1,0:T(8,128)(2,1)} reshape(bf16[64,4,4,512]{3,2,1,0:T(4,128)(2,1)} %get-tuple-element.5) | data formatting | bytes 2097152 | tf_op jit(solution)/shard_map/reshape | solution.py:32
  152.2 0.0 copy-done
  152.3 7.2 %bitcast_reduce_fusion = f32[64,512]{1,0:T(8,128)S(1)} fusion(f32[1024,512]{1,0:T(8,128)} %fusion.1, f32[1024,512]{1,0:T(8,128)} %fusion.3, f32[1024,512]{1,0:T(8,128)} %fusion.5, f32[1024,512]{1,0:T(8,128)S(1)} %copy-done, f32[1024,512]{1,0:T(8,128)} %fusion.9, f32[1024,512]{1,0:T(8,128)} %fusion.11, f32[1024,512]{1,0:T(8,128)} %fusion.15, ...), kind=kOutput, calls=%fused_computation.16 | convolution fusion | flops 543129600 | bytes 19529728 | tf_op jit(solution)/shard_map/dot_general | solution.py:35
  159.5 0.0 copy-done.9
  159.5 0.2 select_reduce_fusion
  159.8 0.7 copy.10
  160.5 0.0 all-to-all-done.2
  160.5 10.3 %all-to-all-start.1 = ((f32[1,64,1]{2,0,1:T(1,128)}), f32[1,64,1]{2,0,1:T(1,128)S(1)}, u32[]{:S(2)}, u32[]{:S(2)}) async-start(f32[1,64,1]{2,0,1:T(1,128)} %copy.10), calls=%async_computation.1 | async-start | bytes 65536 | tf_op jit(solution)/shard_map/all_to_all | solution.py:78
  170.8 1.2 reduce.6
  172.0 8.1 %all-to-all-done.1 = f32[1,64,1]{2,0,1:T(1,128)S(1)} async-done(((f32[1,64,1]{2,0,1:T(1,128)}), f32[1,64,1]{2,0,1:T(1,128)S(1)}, u32[]{:S(2)}, u32[]{:S(2)}) %all-to-all-start.1) | async-done | bytes 288 | tf_op jit(solution)/shard_map/all_to_all | solution.py:78
  180.1 0.7 reduce_sum.28
  181.4 0.7 multiply_reduce_fusion
  182.8 0.6 divide_reduce_fusion
  183.4 0.8 fusion.52
  (12 shorter events, 0.0 us)
Async XLA Ops:
  2.8 41.7 %all-to-all-start = ((bf16[64,1,4,4,512]{4,3,2,1,0:T(4,128)(2,1)}), bf16[64,1,4,4,512]{4,3,2,1,0:T(4,128)(2,1)S(1)}, u32[]{:S(2)}, u32[]{:S(2)}) async-start(bf16[64,1,4,4,512]{4,3,2,1,0:T(4,128)(2,1)} %broadcast_in_dim.30), calls=%async_computation | async-start | bytes 2097152 | tf_op jit(solution)/shard_map/all_to_all | solution.py:17
  45.1 115.3 %all-to-all-start.2 = ((s32[64,1,1]{2,1,0:T(1,128)}), s32[64,1,1]{2,1,0:T(1,128)S(1)}, u32[]{:S(2)}, u32[]{:S(2)}) async-start(s32[64,1,1]{2,1,0:T(1,128)} %broadcast_in_dim.34), calls=%async_computation.2 | async-start | bytes 65536 | tf_op jit(solution)/shard_map/all_to_all | solution.py:17
  61.5 3.5 %copy-start.7 = (bf16[1024,512]{1,0:T(8,128)(2,1)S(1)}, bf16[1024,512]{1,0:T(8,128)(2,1)}, u32[]{:S(2)}) copy-start(bf16[1024,512]{1,0:T(8,128)(2,1)} %reshape.189) | copy-start | bytes 3145732
  95.4 1.9 %copy-start.1 = (f32[1024,512]{1,0:T(8,128)S(1)}, f32[1024,512]{1,0:T(8,128)}, u32[]{:S(2)}) copy-start(f32[1024,512]{1,0:T(8,128)} %fusion.18) | copy-start | bytes 6291460
  116.0 3.2 %copy-start.8 = (bf16[1024,512]{1,0:T(8,128)(2,1)S(1)}, bf16[1024,512]{1,0:T(8,128)(2,1)}, u32[]{:S(2)}) copy-start(bf16[1024,512]{1,0:T(8,128)(2,1)} %reshape.199) | copy-start | bytes 3145732
  119.2 3.1 %copy-start.6 = (bf16[64,4,4,512]{3,2,1,0:T(4,128)(2,1)S(1)}, bf16[64,4,4,512]{3,2,1,0:T(4,128)(2,1)}, u32[]{:S(2)}) copy-start(bf16[64,4,4,512]{3,2,1,0:T(4,128)(2,1)} %get-tuple-element.7) | copy-start | bytes 3145732
  123.4 3.5 %copy-start.5 = (bf16[64,4,4,512]{3,2,1,0:T(4,128)(2,1)S(1)}, bf16[64,4,4,512]{3,2,1,0:T(4,128)(2,1)}, u32[]{:S(2)}) copy-start(bf16[64,4,4,512]{3,2,1,0:T(4,128)(2,1)} %get-tuple-element.6) | copy-start | bytes 3145732
  128.1 3.5 %copy-start.4 = (bf16[64,4,4,512]{3,2,1,0:T(4,128)(2,1)S(1)}, bf16[64,4,4,512]{3,2,1,0:T(4,128)(2,1)}, u32[]{:S(2)}) copy-start(bf16[64,4,4,512]{3,2,1,0:T(4,128)(2,1)} %get-tuple-element.12) | copy-start | bytes 3145732
  132.7 3.6 %copy-start.3 = (bf16[64,4,4,512]{3,2,1,0:T(4,128)(2,1)S(1)}, bf16[64,4,4,512]{3,2,1,0:T(4,128)(2,1)}, u32[]{:S(2)}) copy-start(bf16[64,4,4,512]{3,2,1,0:T(4,128)(2,1)} %get-tuple-element.10) | copy-start | bytes 3145732
  137.4 3.4 %copy-start.2 = (bf16[64,4,4,512]{3,2,1,0:T(4,128)(2,1)S(1)}, bf16[64,4,4,512]{3,2,1,0:T(4,128)(2,1)}, u32[]{:S(2)}) copy-start(bf16[64,4,4,512]{3,2,1,0:T(4,128)(2,1)} %get-tuple-element.9) | copy-start | bytes 3145732
  146.5 5.7 %copy-start = (f32[1024,512]{1,0:T(8,128)S(1)}, f32[1024,512]{1,0:T(8,128)}, u32[]{:S(2)}) copy-start(f32[1024,512]{1,0:T(8,128)} %fusion.7) | copy-start | bytes 6291460
  152.2 7.3 %copy-start.9 = (f32[1,512,10]{1,0,2:T(1,128)S(1)}, f32[1,512,10]{1,0,2:T(1,128)}, u32[]{:S(2)}) copy-start(f32[1,512,10]{1,0,2:T(1,128)} %param.11) | copy-start | bytes 61444
  152.2 7.3 %copy-start.10 = (s32[64]{0:T(128)S(1)}, s32[64]{0:T(128)}, u32[]{:S(2)}) copy-start(s32[64]{0:T(128)} %param.7) | copy-start | bytes 772
  160.5 19.6 %all-to-all-start.1 = ((f32[1,64,1]{2,0,1:T(1,128)}), f32[1,64,1]{2,0,1:T(1,128)S(1)}, u32[]{:S(2)}, u32[]{:S(2)}) async-start(f32[1,64,1]{2,0,1:T(1,128)} %copy.10), calls=%async_computation.1 | async-start | bytes 65536 | tf_op jit(solution)/shard_map/all_to_all | solution.py:78
where the time goes:
time: 187 us; the launch traced here: 186 us
  matrix products  67.3 us (36%)
  local copies, waits for them, and re-layouts  45.3 us (24%)
  waiting for transfers between devices  36 us (19%)
  starting transfers between devices  29.7 us (16%)
  between operations  5.02 us (3%)
  other arithmetic  3.13 us (2%)
    dot_general x18, matrix products, convolve(): jnp.dot(shifted, kernel[offset], preferred_element_type=jnp.float32)  66.3 us
    all_to_all x2, waiting for transfers between devices, sent_to_all(): lax.all_to_all(jnp.broadcast_to(x[None], (devices, *x.shape)), axis, 0, 0...  27.9 us
    reshape x16, local copies, waits for them, and re-layouts, convolve(): padded[:, row_off:row_off + width, col_off:col_off + width, :]  25.5 us
    all_to_all x2, starting transfers between devices, sent_to_all(): lax.all_to_all(jnp.broadcast_to(x[None], (devices, *x.shape)), axis, 0, 0...  19.3 us
    slice x2, local copies, waits for them, and re-layouts, convolve(): padded[:, row_off:row_off + width, col_off:col_off + width, :]  14.8 us
    all_to_all x1, starting transfers between devices, shards(): lax.all_to_all(margin, 'mp', split_axis=1, concat_axis=0, tiled=True)  10.3 us
    all_to_all x1, waiting for transfers between devices, shards(): lax.all_to_all(margin, 'mp', split_axis=1, concat_axis=0, tiled=True)  8.09 us
  transfers between devices with their start and end apart: 3, of which 2 were waited for; matrix products, arithmetic and copies ran while one was open for 59% of the time, Pallas kernels for 0%

commit v1 on v0

v1 whole, which is shorter than its diff:
```python
import functools

import jax
import jax.numpy as jnp
from jax import lax
from jax.experimental import pallas as pl
from jax.experimental.pallas import tpu as pltpu
from jax.sharding import Mesh, PartitionSpec as P

SIDE = 4
SPOTS = SIDE * SIDE
HALF = 256
CLASSES = 10
SUBSETS = 256
GROUP = 16

OFFSETS = (0, 1, 2, 3, 5, 6, 7, 8, 4)


def pairs_of(offset):
    row_off, col_off = offset // 3 - 1, offset % 3 - 1
    return [
        (r * SIDE + c, (r + row_off) * SIDE + c + col_off)
        for r in range(SIDE)
        for c in range(SIDE)
        if 0 <= r + row_off < SIDE and 0 <= c + col_off < SIDE
    ]


def convolve(source, weight, accs):
    stage = 0
    for offset in OFFSETS:
        pairs = pairs_of(offset)
        for k in range(2):
            deep = pl.ds(k * HALF, HALF)
            for n in range(2):
                pltpu.matmul_push_rhs(
                    weight[offset, deep, pl.ds(n * HALF, HALF)], staging_register=stage, mxu_index=n
                )
            for i, (spot, origin) in enumerate(pairs):
                rows = source[origin, :, deep]
                for n in range(2):
                    pltpu.matmul_acc_lhs(
                        accs[n][spot], rows, load_staged_rhs=stage if i == 0 else None
                    )
            stage = 1 - stage


def by_position(sources, moved, accs):
    lane = lax.broadcasted_iota(jnp.int32, (GROUP, HALF), 1)
    target = lax.broadcasted_iota(jnp.int32, (GROUP, HALF), 0)
    picks = [
        jnp.where(lane == target * SPOTS + spot, 1.0, 0.0).astype(jnp.bfloat16)
        for spot in range(SPOTS)
    ]
    pick = jnp.concatenate(picks, axis=0)
    for g, (ref, start) in enumerate(sources):
        for n in range(2):
            pltpu.matmul_push_rhs(
                ref[pl.ds(start, HALF), pl.ds(n * HALF, HALF)], staging_register=g % 2, mxu_index=n
            )
            pltpu.matmul_acc_lhs(accs[n][g], pick, load_staged_rhs=g % 2)
    for g in range(len(sources)):
        for n in range(2):
            got = pltpu.matmul_pop(accs[n][g]).astype(jnp.bfloat16)
            moved[:, pl.ds(g * GROUP, GROUP), pl.ds(n * HALF, HALF)] = got.reshape(SPOTS, GROUP, HALF)


def conv_kernel(core, ident, own, other, w1, w2, head, labels, out, moved, hidden, pooled):
    targets = moved.shape[1]
    groups = targets // GROUP
    sources = [(own, i * HALF) for i in range(groups // 2)] + [(other, i * HALF) for i in range(groups // 2)]

    def shuffle(*flat):
        by_position(sources, moved, (flat[:groups], flat[groups:]))

    pl.run_scoped(
        shuffle,
        *[pltpu.ACC(n)((HALF, HALF), jnp.float32) for n in range(2) for _ in range(groups)],
    )

    def both(*flat):
        accs = (flat[:SPOTS], flat[SPOTS:])
        convolve(moved, w1, accs)
        for spot in range(SPOTS):
            for n in range(2):
                got = jnp.maximum(pltpu.matmul_pop(accs[n][spot]), 0.0)
                hidden[spot, :, pl.ds(n * HALF, HALF)] = got.astype(jnp.bfloat16)
        convolve(hidden, w2, accs)
        for spot in range(SPOTS):
            for n in range(2):
                cols = pl.ds(n * HALF, HALF)
                got = jnp.maximum(pltpu.matmul_pop(accs[n][spot]), 0.0)
                got = got + moved[spot, :, cols].astype(jnp.float32)
                if spot:
                    got = jnp.maximum(got, pooled[:, cols])
                pooled[:, cols] = got

    pl.run_scoped(
        both,
        *[pltpu.ACC(n)((targets, HALF), jnp.float32) for n in range(2) for _ in range(SPOTS)],
    )

    wide = (targets, 128)
    lane = lax.broadcasted_iota(jnp.int32, wide, 1)
    logits = jnp.full(wide, -1e30, jnp.float32)
    for k in range(CLASSES):
        total = pooled[:, pl.ds(0, 128)] * head[pl.ds(k, 1), pl.ds(0, 128)]
        for j in range(1, 4):
            cols = pl.ds(j * 128, 128)
            total = total + pooled[:, cols] * head[pl.ds(k, 1), cols]
        logits = jnp.where(lane == k, jnp.sum(total, axis=1, keepdims=True), logits)
    chosen = lane == labels[...]
    correct = jnp.sum(jnp.where(chosen, logits, 0.0), axis=1, keepdims=True)
    rival = jnp.max(jnp.where(chosen, -1e30, logits), axis=1, keepdims=True)
    ident_f = ident[0].astype(jnp.float32)
    packed = jnp.where(lane < 64, correct - rival, ident_f)
    half = targets // 2
    for j in range(half):
        out[pl.ds(2 * j + core[0], 1), 0, :] = packed[j : j + 1, :]
        out[pl.ds(2 * j + 1 - core[0], 1), 0, :] = packed[half + j : half + j + 1, :]


def conv_call(core, ident, own, other, w1, w2, head, labels):
    targets = 2 * own.shape[0] // SPOTS
    smem = pl.BlockSpec(memory_space=pltpu.SMEM)
    vmem = pl.BlockSpec(memory_space=pltpu.VMEM)
    return pl.pallas_call(
        conv_kernel,
        out_shape=jax.ShapeDtypeStruct((targets, 1, 128), jnp.float32),
        in_specs=[smem, smem] + [vmem] * 6,
        out_specs=vmem,
        scratch_shapes=[
            pltpu.VMEM((SPOTS, targets, 512), jnp.bfloat16),
            pltpu.VMEM((SPOTS, targets, 512), jnp.bfloat16),
            pltpu.VMEM((targets, 512), jnp.float32),
        ],
        compiler_params=pltpu.CompilerParams(vmem_limit_bytes=40 * 1024 * 1024),
        name="margins",
    )(core, ident, own, other, w1, w2, head, labels)


def tail_kernel(columns, datamodel, mean_out, norm_out):
    models = columns.shape[0]
    rows = columns[:, 0, :]
    lane = lax.broadcasted_iota(jnp.int32, rows.shape, 1)
    margin = jnp.max(jnp.where(lane < 64, rows, -3e38), axis=1, keepdims=True)
    ident = jnp.max(jnp.where(lane < 64, -1.0, rows), axis=1, keepdims=True)
    mean = jnp.sum(margin, axis=0, keepdims=True) / models
    centred = margin - mean
    norm = jnp.sqrt(1.0 + jnp.sum(centred * centred, axis=0, keepdims=True) / models)
    scaled = centred / norm
    subset = lax.broadcasted_iota(jnp.int32, (models, SUBSETS), 1).astype(jnp.float32)
    datamodel[...] = jnp.sum(jnp.where(subset == ident, scaled, 0.0), axis=0, keepdims=True)
    mean_out[...] = jnp.broadcast_to(mean, mean_out.shape)
    norm_out[...] = jnp.broadcast_to(norm, norm_out.shape)


def tail_call(columns):
    vmem = pl.BlockSpec(memory_space=pltpu.VMEM)
    return pl.pallas_call(
        tail_kernel,
        out_shape=(
            jax.ShapeDtypeStruct((1, SUBSETS), jnp.float32),
            jax.ShapeDtypeStruct((1, 128), jnp.float32),
            jax.ShapeDtypeStruct((1, 128), jnp.float32),
        ),
        in_specs=[vmem],
        out_specs=(vmem, vmem, vmem),
        name="statistics",
    )(columns)


def exchanged(x, axis):
    return lax.all_to_all(x, axis, 0, 0, tiled=True)


def shards(features, labels, subset_ids, conv1_weight, conv2_weight, head_weight):
    across_z, across_y = lax.axis_size("z"), lax.axis_size("y")
    core = lax.axis_index("core").astype(jnp.int32)
    grid = features.reshape(1, SPOTS, 512)
    column = exchanged(jnp.broadcast_to(grid, (across_z, SPOTS, 512)), "z")
    plane = exchanged(jnp.broadcast_to(column[None], (across_y, *column.shape)), "y")
    own = plane.reshape(-1, 512)
    other = lax.ppermute(own, "core", ((0, 1), (1, 0)))
    pairs = labels.reshape(-1, 2)
    order = jnp.where(core == 0, pairs.T, pairs[:, ::-1].T).reshape(-1, 1)
    wide_labels = jnp.broadcast_to(order, (order.shape[0], 128))
    packed = conv_call(
        core.reshape(1),
        subset_ids,
        own,
        other,
        conv1_weight[0],
        conv2_weight[0],
        head_weight[0].T,
        wide_labels,
    )
    columns = exchanged(packed, ("y", "z", "core"))
    datamodel, mean, norm = tail_call(columns)
    return (datamodel, mean[0, :1], norm[0, :1])


def solution(mesh):
    fine = Mesh(mesh.devices.reshape(4, 8, 2, 4), ("y", "z", "core", "dp"))
    mp = ("y", "z", "core")
    every = ("dp", *mp)
    in_specs = (
        P(every, None, None, None),
        P("dp"),
        P(mp),
        P(mp, None, None, None),
        P(mp, None, None, None),
        P(mp, None, None),
    )
    out_specs = (P(every, None), P(every), P(every))
    return jax.shard_map(shards, mesh=fine, in_specs=in_specs, out_specs=out_specs, check_vma=False)
```

time: 187 us -> 62.6 us (0.33)
  matrix products: 67.3 us -> 0 us
  blocking collectives: 0 us -> 40.8 us
  local copies, waits for them, and re-layouts: 45.3 us -> 7.27 us
  waiting for transfers between devices: 36 us -> 0.01 us
  starting transfers between devices: 29.7 us -> 3.73 us
  Pallas kernels: 0 us -> 8.99 us
  between operations: 5.02 us -> 1.31 us
  other arithmetic: 3.13 us -> 0.01 us
    dot_general x20 -> x0, matrix products: 67.3 us -> none  [the longest x18 66.3 us: convolve(): jnp.dot(shifted, kernel[offset], preferred_element_type=jnp.float32)]
    all_to_all x0 -> x3, blocking collectives: none -> 40.8 us  [exchanged(): return lax.all_to_all(x, axis, 0, 0, tiled=True)]
    all_to_all x3 -> x0, waiting for transfers between devices: 36 us -> none  [the longest x2 27.9 us: sent_to_all(): lax.all_to_all(jnp.broadcast_to(x[None], (devices, *x.shape)), axis, 0, 0...]
    all_to_all x3 -> x0, starting transfers between devices: 29.7 us -> none  [the longest x2 19.3 us: sent_to_all(): lax.all_to_all(jnp.broadcast_to(x[None], (devices, *x.shape)), axis, 0, 0...]
    reshape x18 -> x1, local copies, waits for them, and re-layouts: 26.9 us -> 0.75 us  [shards(): pairs = labels.reshape(-1, 2)]
    slice x2 -> x0, local copies, waits for them, and re-layouts: 14.8 us -> none  [convolve(): padded[:, row_off:row_off + width, col_off:col_off + width, :]]
    pallas_call x0 -> x2, Pallas kernels: none -> 8.99 us  [the longest x1 7.52 us: conv_call(): pl.pallas_call(conv_kernel, out_shape=jax.ShapeDtypeStruct((targets, 1, 1...]
    unnamed x22 -> x5, local copies, waits for them, and re-layouts: 0.04 us -> 5.42 us
  transfers between devices with their start and end apart: 3 -> 1, of which waited for: 2 -> 0; matrix products, arithmetic and copies ran while one was open for 59% -> 3% of each run, Pallas kernels for 0% -> 0%
where the time goes in v1:
time: 62.6 us; the launch traced here: 62.1 us
  blocking collectives  40.8 us (65%)
  Pallas kernels  8.99 us (14%)
  local copies, waits for them, and re-layouts  7.27 us (12%)
  starting transfers between devices  3.73 us (6%)
  between operations  1.31 us (2%)
    all_to_all x3, blocking collectives, exchanged(): return lax.all_to_all(x, axis, 0, 0, tiled=True)  40.8 us
    pallas_call x1, Pallas kernels, conv_call(): pl.pallas_call(conv_kernel, out_shape=jax.ShapeDtypeStruct((targets, 1, 1...  7.52 us
    unnamed x5, local copies, waits for them, and re-layouts  5.42 us
    ppermute x1, starting transfers between devices, shards(): other = lax.ppermute(own, 'core', ((0, 1), (1, 0)))  3.73 us
    pallas_call x1, Pallas kernels, tail_call(): pl.pallas_call(tail_kernel, out_shape=(jax.ShapeDtypeStruct((1, SUBSETS),...  1.48 us
  transfers between devices with their start and end apart: 1, of which 0 were waited for; matrix products, arithmetic and copies ran while one was open for 3% of the time, Pallas kernels for 0%

profile of v1, /device:TPU:1, one launch (start us, length us, event | category | flops | bytes accessed | tf_op | source)
XLA Modules:
  0.0 62.1 jit_solution(3117970970421091804)
XLA Ops:
  0.6 0.7 %broadcast_in_dim.20 = bf16[16,512]{1,0:T(8,128)(2,1)S(1)} reshape(bf16[1,4,4,512]{3,2,1,0:T(4,128)(2,1)} %param.6) | data formatting | bytes 32768 | tf_op jit(solution)/shard_map/broadcast_in_dim | solution.py:182
  1.4 16.6 %all_to_all.15 = bf16[8,16,512]{2,1,0:T(8,128)(2,1)S(1)} all-to-all(bf16[8,16,512]{2,1,0:T(8,128)(2,1)S(1)} %broadcast_in_dim.21), channel_id=1, replica_groups=mesh['y'=4,'z'=8,'core'=2,'dp'=4] {'z'}, dimensions={0} | all-to-all | bytes 262144 | tf_op jit(solution)/shard_map/all_to_all | solution.py:175
  18.0 10.9 %all_to_all.16 = bf16[4,8,16,512]{3,2,1,0:T(8,128)(2,1)S(1)} all-to-all(bf16[4,8,16,512]{3,2,1,0:T(8,128)(2,1)S(1)} %broadcast_in_dim.22), channel_id=1, replica_groups=mesh['y'=4,'z'=8,'core'=2,'dp'=4] {'y'}, dimensions={0} | all-to-all | bytes 1048576 | tf_op jit(solution)/shard_map/all_to_all | solution.py:175
  28.9 3.7 %collective-permute-start = (bf16[512,512]{1,0:T(8,128)(2,1)S(1)}, bf16[512,512]{1,0:T(8,128)(2,1)S(1)}, u32[]{:S(2)}, u32[]{:S(2)}) collective-permute-start(bf16[512,512]{1,0:T(8,128)(2,1)S(1)} %bitcast.17), channel_id=1, source_target_pairs={{0,4},{4,0},{1,5},{5,1},{2,6},{6,2},{3,7},{7,3},{8,12},{12,8},{9,1... | collective-permute-start | bytes 1572872 | tf_op jit(solution)/shard_map/ppermute | solution.py:185
  33.3 0.8 %reshape.22 = s32[32,2]{1,0:T(8,128)S(1)} reshape(s32[64]{0:T(128)} %param.7) | data formatting | bytes 512 | tf_op jit(solution)/shard_map/reshape | solution.py:186
  34.0 0.1 rev.3
  34.1 0.1 copy.10
  34.2 0.1 broadcast_in_dim.23
  34.3 0.7 %copy.13 = f32[1,512,10]{1,2,0:T(8,128)S(1)} copy(f32[1,512,10]{1,0,2:T(1,128)} %param.11) | data formatting | bytes 40960
  35.0 0.0 collective-permute-done.other
  35.0 0.1 broadcast_in_dim.24.labels
  35.1 0.0 copy-start
  35.1 2.3 %copy-done = bf16[1,9,512,512]{3,2,1,0:T(8,128)(2,1)S(1)} copy-done((bf16[1,9,512,512]{3,2,1,0:T(8,128)(2,1)S(1)}, bf16[1,9,512,512]{3,2,1,0:T(8,128)(2,1)}, u32[]{:S(2)}) %copy-start) | copy-done | bytes 4718616
  37.4 0.0 copy-start.1
  37.4 2.3 %copy-done.1 = bf16[1,9,512,512]{3,2,1,0:T(8,128)(2,1)S(1)} copy-done((bf16[1,9,512,512]{3,2,1,0:T(8,128)(2,1)S(1)}, bf16[1,9,512,512]{3,2,1,0:T(8,128)(2,1)}, u32[]{:S(2)}) %copy-start.1) | copy-done | bytes 4718616
  39.8 7.5 %margins.1 = f32[64,1,128]{2,1,0:T(1,128)S(1)} custom-call(s32[1]{0:T(128)} %bitcast.core, s32[1]{0:T(128)S(6)} %copy.14.ident, bf16[512,512]{1,0:T(8,128)(2,1)S(1)} %bitcast.18, bf16[512,512]{1,0:T(8,128)(2,1)S(1)} %collective-permute-done.other, bf16[9,512,512]{2,1,0:T(8,128)(2,1)S(1)} %bitcast.15, bf16[9,512,512]{2,1,0:T(8,128)(2,1)S(1)} %bitcast.16, ...), custom_call_target="tpu_custom_call" | custom-call | tf_op jit(solution)/shard_map/margins/pallas_call | solution.py:128
  47.3 13.3 %all_to_all.17.columns = f32[64,1,128]{2,1,0:T(1,128)} all-to-all(f32[64,1,128]{2,1,0:T(1,128)S(1)} %margins.1), channel_id=1, replica_groups=mesh['y'=4,'z'=8,'core'=2,'dp'=4] {'y','z','core'}, dimensions={0} | all-to-all | bytes 65536 | tf_op jit(solution)/shard_map/all_to_all | solution.py:175
  60.6 1.5 %statistics.1 = (f32[1,256]{1,0:T(1,128)}, f32[1,128]{1,0:T(1,128)}, f32[1,128]{1,0:T(1,128)}) custom-call(f32[64,1,128]{2,1,0:T(1,128)} %all_to_all.17.columns), custom_call_target="tpu_custom_call" | custom-call | tf_op jit(solution)/shard_map/statistics/pallas_call | solution.py:161
  (3 shorter events, 0.1 us)
Async XLA Ops:
  28.9 6.1 %collective-permute-start = (bf16[512,512]{1,0:T(8,128)(2,1)S(1)}, bf16[512,512]{1,0:T(8,128)(2,1)S(1)}, u32[]{:S(2)}, u32[]{:S(2)}) collective-permute-start(bf16[512,512]{1,0:T(8,128)(2,1)S(1)} %bitcast.17), channel_id=1, source_target_pairs={{0,4},{4,0},{1,5},{5,1},{2,6},{6,2},{3,7},{7,3},{8,12},{12,8},{9,1... | collective-permute-start | bytes 1572872 | tf_op jit(solution)/shard_map/ppermute | solution.py:185
  35.1 2.3 %copy-start = (bf16[1,9,512,512]{3,2,1,0:T(8,128)(2,1)S(1)}, bf16[1,9,512,512]{3,2,1,0:T(8,128)(2,1)}, u32[]{:S(2)}) copy-start(bf16[1,9,512,512]{3,2,1,0:T(8,128)(2,1)} %param.9) | copy-start | bytes 14155780
  37.4 2.3 %copy-start.1 = (bf16[1,9,512,512]{3,2,1,0:T(8,128)(2,1)S(1)}, bf16[1,9,512,512]{3,2,1,0:T(8,128)(2,1)}, u32[]{:S(2)}) copy-start(bf16[1,9,512,512]{3,2,1,0:T(8,128)(2,1)} %param.10) | copy-start | bytes 14155780
